TPU v7x, 32 devices: a whole 2x2x4 slice. The times are simulated.
32 devices in a mesh: dp: 8 (over z, x), mp: 4 (over y, core).
Axes of the slice: x: 2, y: 2, z: 4, core: 2. Of those that a mesh axis runs over, the one named last changes fastest.
Arguments:
- teacher_states: bfloat16 [512, 128, 4096], P('dp', None, 'mp'), may hold values from -6 to 6
- teacher_gain: float32 [4096], P('mp'), may hold values from 0.25 to 1.75
- teacher_proj: bfloat16 [4096, 1024], P('mp'), may hold values from -0.09375 to 0.09375
- teacher_mask: int32 [512, 128], P('dp'), may hold values 0 or 1
- student_states: bfloat16 [1024, 64, 768], P(('dp', 'mp')), may hold values from -6 to 6
- student_gain: float32 [768], replicated, may hold values from 0.25 to 1.75
- student_proj: bfloat16 [768, 1024], replicated, may hold values from -0.21875 to 0.21875
- student_mask: int32 [1024, 64], P(('dp', 'mp')), may hold values 0 or 1
- positive: int32 [1024], P(('dp', 'mp')), may hold values from 0 to 511
Outputs:
- grad_embed: float32 [1024, 1024], P(('dp', 'mp'))
- grad_states: bfloat16 [1024, 64, 768], P(('dp', 'mp'))
All inputs are finite; a program needn't handle non-finite values. No bound on the sum of `teacher_mask` or of `student_mask` on one device may be relied on, other than what follows from the above.
Results may differ from a plain program's by a relative error of at most 0.0085.
Values may be sent and summed in bfloat16 or wider, within the bound.
A program may use at most 128 MiB of HBM per device.

v0:
```python
import jax
import jax.numpy as jnp
from jax import lax
from jax.sharding import PartitionSpec as P

D = 4096


def unit_rows(values):
    return (
        values
        * lax.rsqrt(jnp.mean(values * values, axis=-1, keepdims=True) + 1e-06)
        / jnp.sqrt(jnp.float32(values.shape[-1]))
    )


def student_forward(states, gain, proj, live_mask):
    values = states.astype(jnp.float32)
    scale = lax.rsqrt(jnp.mean(values * values, axis=-1, keepdims=True) + 1e-06)
    normed = (values * scale * gain).astype(jnp.bfloat16)
    flat = normed.reshape(-1, normed.shape[-1])
    act = jax.nn.gelu(jnp.dot(flat, proj, preferred_element_type=jnp.float32), approximate=True)
    act = act.reshape(states.shape[0], states.shape[1], -1)
    live = live_mask.astype(jnp.float32)
    pooled = jnp.sum(act * live[:, :, None], axis=1)
    return unit_rows(pooled)


def shards(
    teacher_states,
    teacher_gain,
    teacher_proj,
    teacher_mask,
    student_states,
    student_gain,
    student_proj,
    student_mask,
    positive,
):
    values = teacher_states.astype(jnp.float32)
    partial_squares = jnp.sum(values * values, axis=-1)
    squares = lax.psum(partial_squares, "mp")
    scale = lax.rsqrt(squares / D + 1e-06)
    live = teacher_mask.astype(jnp.float32)
    weight = live * scale
    pooled = jnp.sum(values * weight[:, :, None], axis=1)
    tpooled = (pooled * teacher_gain).astype(jnp.bfloat16)
    partial_embed = jnp.dot(tpooled, teacher_proj, preferred_element_type=jnp.float32)
    summed = lax.psum(partial_embed, "mp")
    group_emb = unit_rows(summed).astype(jnp.bfloat16)
    gathered = lax.all_gather(group_emb, "dp", axis=0, tiled=True)
    semb, back = jax.vjp(
        lambda st: student_forward(st, student_gain, student_proj, student_mask), student_states
    )
    sround = semb.astype(jnp.bfloat16)
    columns = lax.broadcasted_iota(jnp.int32, (positive.shape[0], gathered.shape[0]), 1)
    picker = (positive[:, None] == columns).astype(jnp.bfloat16)
    tpos = jnp.dot(picker, gathered, preferred_element_type=jnp.float32).astype(jnp.bfloat16)
    tlogit = 10.0 * jnp.dot(tpos, gathered.T, preferred_element_type=jnp.float32)
    slogit = 20.0 * jnp.dot(sround, gathered.T, preferred_element_type=jnp.float32)
    texp = jnp.exp(tlogit)
    sexp = jnp.exp(slogit)
    diff = (
        sexp / jnp.sum(sexp, axis=1, keepdims=True) - texp / jnp.sum(texp, axis=1, keepdims=True)
    ).astype(jnp.bfloat16)
    grad_embed = 20.0 * jnp.dot(diff, gathered, preferred_element_type=jnp.float32)
    grad_states = back(grad_embed)[0]
    return (grad_embed, grad_states)


def solution(mesh):
    in_specs = (
        P("dp", None, "mp"),
        P("mp"),
        P("mp", None),
        P("dp", None),
        P(("dp", "mp"), None, None),
        P(),
        P(),
        P(("dp", "mp"), None),
        P(("dp", "mp")),
    )
    out_specs = (P(("dp", "mp"), None), P(("dp", "mp"), None, None))
    return jax.shard_map(shards, mesh=mesh, in_specs=in_specs, out_specs=out_specs, check_vma=False)
```

profile of v0, /device:TPU:0, one launch (start us, length us, event | category | flops | bytes accessed | tf_op | source)
XLA Modules:
  0.0 156.2 jit_solution(10778247551571147130)
XLA Ops:
  7.2 0.0 all-reduce.2.cloned.1.call-start
  7.2 7.4 %fusion = f32[64,128]{1,0:T(8,128)S(1)} fusion(bf16[64,128,1024]{2,1,0:T(8,128)(2,1)} %param.9), kind=kLoop, calls=%fused_computation.2 | loop fusion | flops 25157632 | bytes 16809984 | tf_op jit(solution)/shard_map/reduce_sum | solution.py:41
  14.6 12.9 %psum.14 = f32[64,128]{1,0:T(8,128)S(1)} all-reduce(f32[64,128]{1,0:T(8,128)S(1)} %fusion), channel_id=1, replica_groups=mesh['dp'=8,'mp'=4] {'mp'}, use_global_device_ids=true, to_apply=%region_4.0 | all-reduce | flops 8192 | bytes 65536 | tf_op jit(solution)/shard_map/psum | solution.py:42
  27.6 7.6 %fusion.1 = f32[64,1024]{1,0:T(8,128)S(1)} fusion(bf16[64,128,1024]{2,1,0:T(8,128)(2,1)} %param.9, f32[64,128]{1,0:T(8,128)S(1)} %rsqrt_multiply_fusion), kind=kLoop, calls=%fused_computation.3 | loop fusion | flops 25100288 | bytes 17072128 | tf_op jit(solution)/shard_map/reduce_sum | solution.py:46
  35.3 1.2 fusion.31
  36.5 0.0 all-gather.2.cloned.1.call-start
  36.6 32.7 %all-reduce.2.cloned.1.call-done = f32[64,1024]{1,0:T(8,128)} async-done(((f32[64,1024]{1,0:T(8,128)}), f32[64,1024]{1,0:T(8,128)}) %all-reduce.2.cloned.1.call-update) | async-done | bytes 262160 | tf_op jit(solution)/shard_map/psum | solution.py:49
  69.2 1.1 multiply_reduce_fusion.1
  70.3 1.7 %multiply_convert_fusion = bf16[64,1024]{1,0:T(8,128)(2,1)} fusion(f32[64,1024]{1,0:T(8,128)} %all-reduce.2.cloned.1.call-done, f32[64]{0:T(128)S(1)} %add_rsqrt_fusion), kind=kLoop, calls=%fused_computation.43 | loop fusion | flops 196608 | bytes 393472 | tf_op jit(solution)/shard_map/convert_element_type | solution.py:50
  72.1 0.1 mul.250
  72.2 2.7 %fusion.17 = f32[32,64]{1,0:T(8,128)S(1)} fusion(bf16[32,64,768]{2,1,0:T(8,128)(2,1)} %param.13), kind=kLoop, calls=%fused_computation.28 | loop fusion | flops 4716544 | bytes 3153920 | tf_op jit(solution)/shard_map/jvp()/reduce_sum | solution.py:19
  74.9 2.7 %fusion.19 = bf16[32,64,768]{2,1,0:T(8,128)(2,1)S(1)} fusion(bf16[32,64,768]{2,1,0:T(8,128)(2,1)} %param.13, f32[768]{0:T(1024)S(1)} %copy-done.5, f32[32,64]{1,0:T(8,128)S(1)} %fusion.40), kind=kLoop, calls=%fused_computation.30 | loop fusion | flops 6291456 | bytes 6302720 | tf_op jit(solution)/shard_map/jvp()/convert_element_type | solution.py:20
  77.6 7.7 %multiply_reduce_fusion = (f32[32,1024]{1,0:T(8,128)S(1)}, f32[2048,1024]{1,0:T(8,128)}) fusion(f32[32,64]{1,0:T(8,128)S(1)} %convert_element_type.45, bf16[2048,768]{1,0:T(8,128)(2,1)S(1)} %bitcast.31, bf16[768,1024]{1,0:T(8,128)(2,1)S(1)} %copy-done.3), kind=kOutput, calls=%fused_computation.25 | convolution fusion | flops 3242164224 | bytes 13246464 | tf_op jit(solution)/shard_map/jvp()/dot_general | solution.py:22
  85.3 0.1 multiply_reduce_fusion.3
  85.4 27.1 %all-gather.2.cloned.1.call-done = bf16[512,1024]{1,0:T(8,128)(2,1)} async-done(((bf16[64,1024]{1,0:T(8,128)(2,1)}), bf16[512,1024]{1,0:T(8,128)(2,1)}) %all-gather.2.cloned.1.call-update) | async-done | bytes 1048592 | tf_op jit(solution)/shard_map/all_gather | solution.py:51
  112.5 2.5 %fusion.45 = (f32[32]{0:T(128)S(1)}, f32[32,512]{1,0:T(8,128)S(1)}) fusion(bf16[512,1024]{1,0:T(8,128)(2,1)} %all-gather.2.cloned.1.call-done, s32[32]{0:T(128)S(1)} %copy-done.9), kind=kOutput, calls=%fused_computation.73 | convolution fusion | flops 67190752 | bytes 1114368 | tf_op jit(solution)/shard_map/dot_general | solution.py:59
  115.0 1.8 %fusion.46 = (f32[32]{0:T(128)S(1)}, f32[32,512]{1,0:T(8,128)S(1)}) fusion(bf16[512,1024]{1,0:T(8,128)(2,1)} %all-gather.2.cloned.1.call-done, f32[32,1024]{1,0:T(8,128)S(1)} %get-tuple-element.8, f32[32]{0:T(128)S(1)} %fusion.41), kind=kOutput, calls=%fused_computation.74 | convolution fusion | flops 33685472 | bytes 1245440 | tf_op jit(solution)/shard_map/dot_general | solution.py:60
  116.7 1.7 %multiply_reduce_fusion.2 = (f32[32]{0:T(128)S(1)}, f32[32,1024]{1,0:T(8,128)S(1)}) fusion(f32[32,1024]{1,0:T(8,128)S(1)} %get-tuple-element.8, bf16[512,1024]{1,0:T(8,128)(2,1)} %all-gather.2.cloned.1.call-done, f32[32,512]{1,0:T(8,128)S(1)} %get-tuple-element.11, f32[32,512]{1,0:T(8,128)S(1)} %get-tuple-element.13, f32[32]{0:T(128)S(1)} %get-tuple-element.10, ...), kind=kOutput, calls=%fused_computation.48 | convolution fusion | flops 33718240 | bytes 1442176 | tf_op jit(solution)/shard_map/dot_general | solution.py:66
  118.4 0.7 add_add_fusion.1
  119.1 11.1 %fusion.14 = (f32[2048,1024]{1,0:T(8,128)}, f32[2048,1024]{1,0:T(8,128)}) fusion(f32[2048,1024]{1,0:T(8,128)} %get-tuple-element.9, f32[2048]{0:T(1024)S(1)} %mul.250, f32[32,1024]{1,0:T(8,128)S(1)} %get-tuple-element.4), kind=kLoop, calls=%fused_computation.23 | loop fusion | flops 33554432 | bytes 25305088 | tf_op jit(solution)/shard_map/transpose(jvp())/mul | solution.py:22
  130.2 11.6 %fusion.24 = bf16[2048,768]{1,0:T(8,128)(2,1)} fusion(bf16[768,1024]{1,0:T(8,128)(2,1)S(1)} %copy-done.4, f32[2048,1024]{1,0:T(8,128)} %get-tuple-element.3, f32[2048,1024]{1,0:T(8,128)S(1)} %bitcast.29, f32[2048,1024]{1,0:T(8,128)} %get-tuple-element.2), kind=kOutput, calls=%fused_computation.36 | convolution fusion | flops 3233284096 | bytes 29884416 | tf_op jit(solution)/shard_map/transpose(jvp())/dot_general | solution.py:22
  141.9 4.1 %fusion.20 = f32[32,64]{1,0:T(8,128)S(1)} fusion(bf16[32,64,768]{2,1,0:T(8,128)(2,1)} %param.13, bf16[32,64,768]{2,1,0:T(8,128)(2,1)} %bitcast.30, f32[768]{0:T(1024)S(1)} %copy-done.5), kind=kLoop, calls=%fused_computation.31 | loop fusion | flops 7862272 | bytes 6302720 | tf_op jit(solution)/shard_map/transpose(jvp())/reduce_sum | solution.py:20
  146.0 0.6 copy-done.2
  146.6 2.8 %fusion.16 = bf16[32,64,768]{2,1,0:T(8,128)(2,1)} fusion(bf16[32,64,768]{2,1,0:T(8,128)(2,1)S(1)} %copy-done.1, f32[32,64]{1,0:T(8,128)S(1)} %multiply_multiply_fusion.3, f32[768]{0:T(1024)S(1)} %copy-done.5, f32[32,64]{1,0:T(8,128)S(1)} %fusion.40, bf16[2048,768]{1,0:T(8,128)(2,1)S(1)} %copy-done.2), kind=kLoop, calls=%fused_computation.27 | loop fusion | flops 12582912 | bytes 9456640 | tf_op jit(solution)/shard_map/transpose(jvp())/convert_element_type | solution.py:18
  (33 shorter events, 0.2 us)
Async XLA Ops:
  7.2 28.1 %copy-start = (bf16[1024,1024]{1,0:T(8,128)(2,1)S(1)}, bf16[1024,1024]{1,0:T(8,128)(2,1)}, u32[]{:S(2)}) copy-start(bf16[1024,1024]{1,0:T(8,128)(2,1)} %param.11) | copy-start | bytes 6291460
  7.2 20.4 %copy-start.6 = (s32[64,128]{1,0:T(8,128)S(1)}, s32[64,128]{1,0:T(8,128)}, u32[]{:S(2)}) copy-start(s32[64,128]{1,0:T(8,128)} %param.12) | copy-start | bytes 98308
  7.2 62.1 %all-reduce.2.cloned.1.call-start = ((), (), s32[]{:S(2)}) async-start(), calls=%async_computation | async-start | bytes 524288 | tf_op jit(solution)/shard_map/psum | solution.py:49
  27.6 7.7 %copy-start.8 = (f32[1024]{0:T(1024)S(1)}, f32[1024]{0:T(1024)}, u32[]{:S(2)}) copy-start(f32[1024]{0:T(1024)} %param.10) | copy-start | bytes 12292
  27.6 44.5 %copy-start.7 = (s32[32,64]{1,0:T(8,128)S(1)}, s32[32,64]{1,0:T(8,128)}, u32[]{:S(2)}) copy-start(s32[32,64]{1,0:T(8,128)} %param.16) | copy-start | bytes 24580
  27.6 47.2 %copy-start.5 = (f32[768]{0:T(1024)S(1)}, f32[768]{0:T(1024)}, u32[]{:S(2)}) copy-start(f32[768]{0:T(1024)} %param.14) | copy-start | bytes 9220
  36.5 76.0 %all-gather.2.cloned.1.call-start = ((), (), s32[]{:S(2)}) async-start(), calls=%async_computation.1 | async-start | bytes 1179648 | tf_op jit(solution)/shard_map/all_gather | solution.py:51
  72.2 5.4 %copy-start.3 = (bf16[768,1024]{1,0:T(8,128)(2,1)S(1)}, bf16[768,1024]{1,0:T(8,128)(2,1)}, u32[]{:S(2)}) copy-start(bf16[768,1024]{1,0:T(8,128)(2,1)} %param.15) | copy-start | bytes 4718596
  74.9 37.6 %copy-start.9 = (s32[32]{0:T(128)S(1)}, s32[32]{0:T(128)}, u32[]{:S(2)}) copy-start(s32[32]{0:T(128)} %param.17) | copy-start | bytes 388
  118.4 11.8 %slice-start = ((s8[8388608]{0:T(1024)(128)(4,1)}), s8[4194304]{0:T(1024)(128)(4,1)S(1)}, s32[]{:S(2)}) async-start(s8[8388608]{0:T(1024)(128)(4,1)} %bitcast.28), calls=%async_computation.2 | async-start | bytes 8388608
  119.1 11.1 %slice-start.1 = ((s8[8388608]{0:T(1024)(128)(4,1)}), s8[4194304]{0:T(1024)(128)(4,1)S(1)}, s32[]{:S(2)}) async-start(s8[8388608]{0:T(1024)(128)(4,1)} %bitcast.28), calls=%async_computation.3 | async-start | bytes 8388608
  119.1 11.1 %copy-start.4 = (bf16[768,1024]{1,0:T(8,128)(2,1)S(1)}, bf16[768,1024]{1,0:T(8,128)(2,1)}, u32[]{:S(2)}) copy-start(bf16[768,1024]{1,0:T(8,128)(2,1)} %param.15) | copy-start | bytes 4718596
  141.9 4.1 %copy-start.1 = (bf16[32,64,768]{2,1,0:T(8,128)(2,1)S(1)}, bf16[32,64,768]{2,1,0:T(8,128)(2,1)}, u32[]{:S(2)}) copy-start(bf16[32,64,768]{2,1,0:T(8,128)(2,1)} %param.13) | copy-start | bytes 9437188
  141.9 4.7 %copy-start.2 = (bf16[2048,768]{1,0:T(8,128)(2,1)S(1)}, bf16[2048,768]{1,0:T(8,128)(2,1)}, u32[]{:S(2)}) copy-start(bf16[2048,768]{1,0:T(8,128)(2,1)} %fusion.24) | copy-start | bytes 9437188
Sparse Core Ops, SparseCore 0:
  36.6 32.5 all-reduce.1
  72.2 40.2 all-gather.1
where the time goes:
time: 157 us; the launch traced here: 156 us
  waiting for transfers between devices  59.8 us (38%)
  other arithmetic  41.9 us (27%)
  matrix products  26.5 us (17%)
  between operations  14.2 us (9%)
  blocking collectives  12.9 us (8%)
    psum x1, waiting for transfers between devices, shards(): summed = lax.psum(partial_embed, 'mp')  32.7 us
    all_gather x1, waiting for transfers between devices, shards(): gathered = lax.all_gather(group_emb, 'dp', axis=0, tiled=True)  27.1 us
    dot_general x2, matrix products, student_forward(): jnp.dot(flat, proj, preferred_element_type=jnp.float32)  19.3 us
    psum x1, blocking collectives, shards(): squares = lax.psum(partial_squares, 'mp')  12.9 us
    mul x1, other arithmetic, student_forward(): jax.nn.gelu(jnp.dot(flat, proj, preferred_element_type=jnp.float32), appr...  11.1 us
    reduce_sum x1, other arithmetic, shards(): pooled = jnp.sum(values * weight[:, :, None], axis=1)  7.65 us
    reduce_sum x1, other arithmetic, shards(): partial_squares = jnp.sum(values * values, axis=-1)  7.38 us
    reduce_sum x1, other arithmetic, student_forward(): normed = (values * scale * gain).astype(jnp.bfloat16)  4.07 us
  transfers between devices with their start and end apart: 2, of which 2 were waited for; matrix products, arithmetic and copies ran while one was open for 8% of the time, Pallas kernels for 0%

commit v1 on v0

--- a/solution.py
+++ b/solution.py
@@ -46,7 +46,8 @@
     pooled = jnp.sum(values * weight[:, :, None], axis=1)
     tpooled = (pooled * teacher_gain).astype(jnp.bfloat16)
     partial_embed = jnp.dot(tpooled, teacher_proj, preferred_element_type=jnp.float32)
-    summed = lax.psum(partial_embed, "mp")
+    blocks = lax.all_gather(partial_embed, "mp")
+    summed = jnp.sum(blocks, axis=0)
     group_emb = unit_rows(summed).astype(jnp.bfloat16)
     gathered = lax.all_gather(group_emb, "dp", axis=0, tiled=True)
     semb, back = jax.vjp(

time: 157 us -> 141 us (0.90)
  waiting for transfers between devices: 59.8 us -> 44.6 us
    psum x1 -> x0, waiting for transfers between devices: 32.7 us -> none  [shards(): summed = lax.psum(partial_embed, 'mp')]
    all_gather x0 -> x1, waiting for transfers between devices: none -> 17.1 us  [shards(): blocks = lax.all_gather(partial_embed, 'mp')]
  transfers between devices with their start and end apart: 2 -> 2, of which waited for: 2 -> 2; matrix products, arithmetic and copies ran while one was open for 8% -> 9% of each run, Pallas kernels for 0% -> 0%
where the time goes in v1:
time: 141 us; the launch traced here: 140 us
  waiting for transfers between devices  44.6 us (32%)
  other arithmetic  41.4 us (29%)
  matrix products  26.4 us (19%)
  between operations  14.2 us (10%)
  blocking collectives  12.9 us (9%)
    all_gather x1, waiting for transfers between devices, shards(): gathered = lax.all_gather(group_emb, 'dp', axis=0, tiled=True)  27.5 us
    dot_general x2, matrix products, student_forward(): jnp.dot(flat, proj, preferred_element_type=jnp.float32)  19.3 us
    all_gather x1, waiting for transfers between devices, shards(): blocks = lax.all_gather(partial_embed, 'mp')  17.1 us
    psum x1, blocking collectives, shards(): squares = lax.psum(partial_squares, 'mp')  12.9 us
    mul x1, other arithmetic, student_forward(): jax.nn.gelu(jnp.dot(flat, proj, preferred_element_type=jnp.float32), appr...  11.1 us
    reduce_sum x1, other arithmetic, shards(): pooled = jnp.sum(values * weight[:, :, None], axis=1)  7.65 us
    reduce_sum x1, other arithmetic, shards(): partial_squares = jnp.sum(values * values, axis=-1)  7.38 us
    reduce_sum x1, other arithmetic, student_forward(): normed = (values * scale * gain).astype(jnp.bfloat16)  4.07 us
  transfers between devices with their start and end apart: 2, of which 2 were waited for; matrix products, arithmetic and copies ran while one was open for 9% of the time, Pallas kernels for 0%

profile of v1, /device:TPU:0, one launch (start us, length us, event | category | flops | bytes accessed | tf_op | source)
XLA Modules:
  0.0 140.4 jit_solution(2609986423839235895)
XLA Ops:
  7.2 7.4 %fusion = f32[64,128]{1,0:T(8,128)S(1)} fusion(bf16[64,128,1024]{2,1,0:T(8,128)(2,1)} %param.9), kind=kLoop, calls=%fused_computation.2 | loop fusion | flops 25157632 | bytes 16809984 | tf_op jit(solution)/shard_map/reduce_sum | solution.py:41
  14.6 12.9 %psum.7 = f32[64,128]{1,0:T(8,128)S(1)} all-reduce(f32[64,128]{1,0:T(8,128)S(1)} %fusion), channel_id=1, replica_groups=mesh['dp'=8,'mp'=4] {'mp'}, use_global_device_ids=true, to_apply=%region_4.0 | all-reduce | flops 8192 | bytes 65536 | tf_op jit(solution)/shard_map/psum | solution.py:42
  27.6 7.6 %fusion.1 = f32[64,1024]{1,0:T(8,128)S(1)} fusion(bf16[64,128,1024]{2,1,0:T(8,128)(2,1)} %param.9, f32[64,128]{1,0:T(8,128)S(1)} %rsqrt_multiply_fusion), kind=kLoop, calls=%fused_computation.3 | loop fusion | flops 25100288 | bytes 17072128 | tf_op jit(solution)/shard_map/reduce_sum | solution.py:46
  35.3 1.2 fusion.31
  36.5 0.0 all-gather.4.cloned.1.call-start
  36.6 17.1 %all-gather.6.cloned.1.call-done = f32[256,1024]{1,0:T(8,128)} async-done(((f32[64,1024]{1,0:T(8,128)}), f32[256,1024]{1,0:T(8,128)}) %all-gather.6.cloned.1.call-update) | async-done | bytes 1048592 | tf_op jit(solution)/shard_map/all_gather | solution.py:49
  53.7 1.3 reduce_sum.112
  55.0 0.1 multiply_reduce_fusion.1
  55.1 0.8 multiply_convert_fusion
  55.9 0.1 mul.250
  56.0 2.7 %fusion.17 = f32[32,64]{1,0:T(8,128)S(1)} fusion(bf16[32,64,768]{2,1,0:T(8,128)(2,1)} %param.13), kind=kLoop, calls=%fused_computation.28 | loop fusion | flops 4716544 | bytes 3153920 | tf_op jit(solution)/shard_map/jvp()/reduce_sum | solution.py:19
  58.7 2.7 %fusion.19 = bf16[32,64,768]{2,1,0:T(8,128)(2,1)S(1)} fusion(bf16[32,64,768]{2,1,0:T(8,128)(2,1)} %param.13, f32[768]{0:T(1024)S(1)} %copy-done.5, f32[32,64]{1,0:T(8,128)S(1)} %fusion.40), kind=kLoop, calls=%fused_computation.30 | loop fusion | flops 6291456 | bytes 6302720 | tf_op jit(solution)/shard_map/jvp()/convert_element_type | solution.py:20
  61.4 7.7 %multiply_reduce_fusion = (f32[32,1024]{1,0:T(8,128)S(1)}, f32[2048,1024]{1,0:T(8,128)}) fusion(f32[32,64]{1,0:T(8,128)S(1)} %convert_element_type.45, bf16[2048,768]{1,0:T(8,128)(2,1)S(1)} %bitcast.32, bf16[768,1024]{1,0:T(8,128)(2,1)S(1)} %copy-done.3), kind=kOutput, calls=%fused_computation.25 | convolution fusion | flops 3242164224 | bytes 13246464 | tf_op jit(solution)/shard_map/jvp()/dot_general | solution.py:22
  69.1 0.1 multiply_reduce_fusion.3
  69.2 27.5 %all-gather.4.cloned.1.call-done = bf16[512,1024]{1,0:T(8,128)(2,1)} async-done(((bf16[64,1024]{1,0:T(8,128)(2,1)}), bf16[512,1024]{1,0:T(8,128)(2,1)}) %all-gather.4.cloned.1.call-update) | async-done | bytes 1048592 | tf_op jit(solution)/shard_map/all_gather | solution.py:52
  96.7 2.5 %fusion.45 = (f32[32]{0:T(128)S(1)}, f32[32,512]{1,0:T(8,128)S(1)}) fusion(bf16[512,1024]{1,0:T(8,128)(2,1)} %all-gather.4.cloned.1.call-done, s32[32]{0:T(128)S(1)} %copy-done.9), kind=kOutput, calls=%fused_computation.73 | convolution fusion | flops 67190752 | bytes 1114368 | tf_op jit(solution)/shard_map/dot_general | solution.py:60
  99.2 1.8 %fusion.46 = (f32[32]{0:T(128)S(1)}, f32[32,512]{1,0:T(8,128)S(1)}) fusion(bf16[512,1024]{1,0:T(8,128)(2,1)} %all-gather.4.cloned.1.call-done, f32[32,1024]{1,0:T(8,128)S(1)} %get-tuple-element.8, f32[32]{0:T(128)S(1)} %fusion.41), kind=kOutput, calls=%fused_computation.74 | convolution fusion | flops 33685472 | bytes 1245440 | tf_op jit(solution)/shard_map/dot_general | solution.py:61
  100.9 1.7 %multiply_reduce_fusion.2 = (f32[32]{0:T(128)S(1)}, f32[32,1024]{1,0:T(8,128)S(1)}) fusion(f32[32,1024]{1,0:T(8,128)S(1)} %get-tuple-element.8, bf16[512,1024]{1,0:T(8,128)(2,1)} %all-gather.4.cloned.1.call-done, f32[32,512]{1,0:T(8,128)S(1)} %get-tuple-element.11, f32[32,512]{1,0:T(8,128)S(1)} %get-tuple-element.13, f32[32]{0:T(128)S(1)} %get-tuple-element.10, ...), kind=kOutput, calls=%fused_computation.48 | convolution fusion | flops 33718240 | bytes 1442176 | tf_op jit(solution)/shard_map/dot_general | solution.py:67
  102.6 0.7 add_add_fusion.1
  103.3 11.1 %fusion.14 = (f32[2048,1024]{1,0:T(8,128)}, f32[2048,1024]{1,0:T(8,128)}) fusion(f32[2048,1024]{1,0:T(8,128)} %get-tuple-element.9, f32[2048]{0:T(1024)S(1)} %mul.250, f32[32,1024]{1,0:T(8,128)S(1)} %get-tuple-element.4), kind=kLoop, calls=%fused_computation.23 | loop fusion | flops 33554432 | bytes 25305088 | tf_op jit(solution)/shard_map/transpose(jvp())/mul | solution.py:22
  114.4 11.6 %fusion.24 = bf16[2048,768]{1,0:T(8,128)(2,1)} fusion(bf16[768,1024]{1,0:T(8,128)(2,1)S(1)} %copy-done.4, f32[2048,1024]{1,0:T(8,128)} %get-tuple-element.3, f32[2048,1024]{1,0:T(8,128)S(1)} %bitcast.30, f32[2048,1024]{1,0:T(8,128)} %get-tuple-element.2), kind=kOutput, calls=%fused_computation.36 | convolution fusion | flops 3233284096 | bytes 29884416 | tf_op jit(solution)/shard_map/transpose(jvp())/dot_general | solution.py:22
  126.1 4.1 %fusion.20 = f32[32,64]{1,0:T(8,128)S(1)} fusion(bf16[32,64,768]{2,1,0:T(8,128)(2,1)} %param.13, bf16[32,64,768]{2,1,0:T(8,128)(2,1)} %bitcast.31, f32[768]{0:T(1024)S(1)} %copy-done.5), kind=kLoop, calls=%fused_computation.31 | loop fusion | flops 7862272 | bytes 6302720 | tf_op jit(solution)/shard_map/transpose(jvp())/reduce_sum | solution.py:20
  130.2 0.6 copy-done.2
  130.8 2.8 %fusion.16 = bf16[32,64,768]{2,1,0:T(8,128)(2,1)} fusion(bf16[32,64,768]{2,1,0:T(8,128)(2,1)S(1)} %copy-done.1, f32[32,64]{1,0:T(8,128)S(1)} %multiply_multiply_fusion.3, f32[768]{0:T(1024)S(1)} %copy-done.5, f32[32,64]{1,0:T(8,128)S(1)} %fusion.40, bf16[2048,768]{1,0:T(8,128)(2,1)S(1)} %copy-done.2), kind=kLoop, calls=%fused_computation.27 | loop fusion | flops 12582912 | bytes 9456640 | tf_op jit(solution)/shard_map/transpose(jvp())/convert_element_type | solution.py:18
  (34 shorter events, 0.2 us)
Async XLA Ops:
  7.2 28.1 %copy-start = (bf16[1024,1024]{1,0:T(8,128)(2,1)S(1)}, bf16[1024,1024]{1,0:T(8,128)(2,1)}, u32[]{:S(2)}) copy-start(bf16[1024,1024]{1,0:T(8,128)(2,1)} %param.11) | copy-start | bytes 6291460
  7.2 20.4 %copy-start.6 = (s32[64,128]{1,0:T(8,128)S(1)}, s32[64,128]{1,0:T(8,128)}, u32[]{:S(2)}) copy-start(s32[64,128]{1,0:T(8,128)} %param.12) | copy-start | bytes 98308
  7.2 46.5 %all-gather.6.cloned.1.call-start = ((), (), s32[]{:S(2)}) async-start(), calls=%async_computation.1 | async-start | bytes 1310720 | tf_op jit(solution)/shard_map/all_gather | solution.py:49
  27.6 7.7 %copy-start.8 = (f32[1024]{0:T(1024)S(1)}, f32[1024]{0:T(1024)}, u32[]{:S(2)}) copy-start(f32[1024]{0:T(1024)} %param.10) | copy-start | bytes 12292
  27.6 28.3 %copy-start.7 = (s32[32,64]{1,0:T(8,128)S(1)}, s32[32,64]{1,0:T(8,128)}, u32[]{:S(2)}) copy-start(s32[32,64]{1,0:T(8,128)} %param.16) | copy-start | bytes 24580
  27.6 31.1 %copy-start.5 = (f32[768]{0:T(1024)S(1)}, f32[768]{0:T(1024)}, u32[]{:S(2)}) copy-start(f32[768]{0:T(1024)} %param.14) | copy-start | bytes 9220
  36.5 60.2 %all-gather.4.cloned.1.call-start = ((), (), s32[]{:S(2)}) async-start(), calls=%async_computation | async-start | bytes 1179648 | tf_op jit(solution)/shard_map/all_gather | solution.py:52
  56.0 5.4 %copy-start.3 = (bf16[768,1024]{1,0:T(8,128)(2,1)S(1)}, bf16[768,1024]{1,0:T(8,128)(2,1)}, u32[]{:S(2)}) copy-start(bf16[768,1024]{1,0:T(8,128)(2,1)} %param.15) | copy-start | bytes 4718596
  58.7 38.0 %copy-start.9 = (s32[32]{0:T(128)S(1)}, s32[32]{0:T(128)}, u32[]{:S(2)}) copy-start(s32[32]{0:T(128)} %param.17) | copy-start | bytes 388
  102.6 11.8 %slice-start = ((s8[8388608]{0:T(1024)(128)(4,1)}), s8[4194304]{0:T(1024)(128)(4,1)S(1)}, s32[]{:S(2)}) async-start(s8[8388608]{0:T(1024)(128)(4,1)} %bitcast.29), calls=%async_computation.2 | async-start | bytes 8388608
  103.3 11.1 %slice-start.1 = ((s8[8388608]{0:T(1024)(128)(4,1)}), s8[4194304]{0:T(1024)(128)(4,1)S(1)}, s32[]{:S(2)}) async-start(s8[8388608]{0:T(1024)(128)(4,1)} %bitcast.29), calls=%async_computation.3 | async-start | bytes 8388608
  103.3 11.1 %copy-start.4 = (bf16[768,1024]{1,0:T(8,128)(2,1)S(1)}, bf16[768,1024]{1,0:T(8,128)(2,1)}, u32[]{:S(2)}) copy-start(bf16[768,1024]{1,0:T(8,128)(2,1)} %param.15) | copy-start | bytes 4718596
  126.1 4.1 %copy-start.1 = (bf16[32,64,768]{2,1,0:T(8,128)(2,1)S(1)}, bf16[32,64,768]{2,1,0:T(8,128)(2,1)}, u32[]{:S(2)}) copy-start(bf16[32,64,768]{2,1,0:T(8,128)(2,1)} %param.13) | copy-start | bytes 9437188
  126.1 4.7 %copy-start.2 = (bf16[2048,768]{1,0:T(8,128)(2,1)S(1)}, bf16[2048,768]{1,0:T(8,128)(2,1)}, u32[]{:S(2)}) copy-start(bf16[2048,768]{1,0:T(8,128)(2,1)} %fusion.24) | copy-start | bytes 9437188
Sparse Core Ops, SparseCore 0:
  36.6 16.9 all-gather.5
  56.4 40.2 all-gather.3
